TPU v7x, 32 devices: a whole 2x2x4 slice. The times are simulated.
32 devices in a mesh: seq: 8 (over z, x), kvh: 4 (over y, core).
Axes of the slice: x: 2, y: 2, z: 4, core: 2. Of those that a mesh axis runs over, the one named last changes fastest.
Arguments:
- queries: bfloat16 [1024, 28, 128], P('seq', 'kvh'), may hold values from -80 to 80
- new_keys: bfloat16 [1024, 4, 128], P('seq', 'kvh'), may hold values from -8 to 8
- cache_keys: bfloat16 [512, 4, 128], P('seq', 'kvh'), may hold values from -1.1953125 to 1.1953125
- window_start: int32 [8], replicated, may hold values from 0 to 512, as said below
- owner_slot: int32 [8], replicated, may hold values from 0 to 511, as said below
Outputs:
- relevance: bfloat16 [1024, 28, 512], P('seq', 'kvh')
- rep_bank: bfloat16 [512, 4, 128], P('seq', 'kvh')
Inputs may be any that keep to these rules, and one draw needn't show every extreme that they name: `window_start`: each window lies inside the new tokens; some window begins at the first new token and some ends at the last. `owner_slot`: the slots are distinct; the first and the last memory block are always among them.
All inputs are finite; a program needn't handle non-finite values.
Results may differ from a plain program's by a relative error of at most 0.0018.
Values may be sent and summed in bfloat16 or wider, within the bound.
A program may use at most 64 MiB of HBM per device.

v0:
```python
import functools
import math

import jax
import jax.numpy as jnp
from jax import lax
from jax.experimental import pallas as pl
from jax.experimental.pallas import tpu as pltpu
from jax.sharding import PartitionSpec as P

BLK = 128
WIN = 512
VMEM = 67043328
LOG2E = 1.4426950408889634
NT = (((1,), (1,)), ((), ()))


def each(count, body):
    if count <= 8:
        for i in range(count):
            body(i)
    else:
        lax.fori_loop(0, count, lambda i, c: (body(i), c)[1], 0)


def refresh_kernel(
    n, start_hbm, slot_hbm, q_hbm, k_hbm, c_hbm, q_v, bank,
    start_ref, slot_ref, q_t, keys, cache, mine, parts,
    load_sem, ks_sem, kr_sem, cs_sem, cr_sem, ps_sem, pr_sem,
):
    group, toks, dim = q_v.shape
    ktoks = keys.shape[1]
    local = cache.shape[1]
    slots = n * local
    per = ktoks // BLK
    blocks = n * per
    rows = group * toks
    scale = 1.0 / math.sqrt(dim)
    me = lax.axis_index("seq")

    load_k = pltpu.make_async_copy(k_hbm, keys.at[me], load_sem.at[0])
    load_q = pltpu.make_async_copy(q_hbm, q_v, load_sem.at[1])
    load_c = pltpu.make_async_copy(c_hbm, cache.at[me], load_sem.at[2])
    load_w = pltpu.make_async_copy(start_hbm, start_ref, load_sem.at[3])
    load_s = pltpu.make_async_copy(slot_hbm, slot_ref, load_sem.at[4])
    load_k.start()
    load_c.start()
    load_q.start()
    load_w.start()
    load_s.start()

    barrier = pltpu.get_barrier_semaphore()

    def greet(i):
        peer = lax.rem(me + 1 + i, n)
        pl.semaphore_signal(
            barrier, inc=1, device_id={"seq": peer}, device_id_type=pl.DeviceIdType.MESH
        )

    each(n - 1, greet)

    def link(src, dst, s_sem, r_sem, peer):
        return pltpu.make_async_remote_copy(
            src_ref=src, dst_ref=dst, send_sem=s_sem, recv_sem=r_sem,
            device_id={"seq": peer}, device_id_type=pl.DeviceIdType.MESH,
        )

    def key_copy(slot, peer):
        return link(keys.at[slot], keys.at[slot], ks_sem.at[peer], kr_sem.at[slot], peer)

    def cache_copy(slot, peer):
        return link(cache.at[slot], cache.at[slot], cs_sem.at[peer], cr_sem.at[slot], peer)

    def part_copy(slot, peer, src):
        return link(src, parts.at[slot], ps_sem.at[peer], pr_sem.at[slot], peer)

    load_q.wait()
    load_w.wait()
    load_s.wait()
    for j in range(group):
        q_t[:, j * toks:(j + 1) * toks] = q_v[j].T

    load_k.wait()
    position = me * toks + lax.broadcasted_iota(jnp.int32, (1, toks), 1)

    def partial(owner):
        for p in range(per):
            index = owner * per + p
            kb = keys[owner, p * BLK:(p + 1) * BLK, :]
            begin = start_ref[index]
            mask = jnp.where((position >= begin) & (position < begin + WIN), 1.0, 0.0)
            s = jnp.dot(kb, q_t[...], preferred_element_type=jnp.float32)
            top = jnp.max(s, axis=0, keepdims=True)
            e = jnp.exp2((s - top) * (scale * LOG2E))
            total = jnp.sum(e, axis=0, keepdims=True)
            acc = None
            for j in range(group):
                cols = slice(j * toks, (j + 1) * toks)
                term = e[:, cols] * (mask / total[:, cols])
                acc = term if acc is None else acc + term
            weight = jnp.sum(acc, axis=1, keepdims=True)
            rep = jnp.sum(weight * kb.astype(jnp.float32), axis=0, keepdims=True)
            mine[pl.ds(index, 1), :] = rep

    partial(me)

    pl.semaphore_wait(barrier, n - 1)
    each(n - 1, lambda i: key_copy(me, lax.rem(me + 1 + i, n)).start())
    load_c.wait()

    def arrive(i):
        owner = lax.rem(me + n - 1 - i, n)
        key_copy(owner, owner).wait_recv()
        partial(owner)

    each(n - 1, arrive)
    each(n - 1, lambda i: part_copy(me, lax.rem(me + 1 + i, n), mine).start())
    each(n - 1, lambda i: cache_copy(me, lax.rem(me + 1 + i, n)).start())

    each(n - 1, lambda i: cache_copy(lax.rem(me + n - 1 - i, n), me).wait_recv())
    hits = jnp.where(
        lax.broadcasted_iota(jnp.int32, (slots, blocks), 0) == slot_ref[...], 1.0, 0.0
    )
    taken = jnp.max(hits, axis=1, keepdims=True)
    hits = hits.astype(jnp.bfloat16)
    old = cache[...].reshape(slots, dim)

    each(n - 1, lambda i: part_copy(lax.rem(me + n - 1 - i, n), me, mine).wait_recv())
    parts[me] = mine[...]
    if n <= 8:
        rep_sum = parts[0]
        for d in range(1, n):
            rep_sum = rep_sum + parts[d]
    else:
        rep_sum = lax.fori_loop(1, n, lambda d, c: c + parts[d], parts[0])
    rep = (rep_sum * (1.0 / (group * WIN))).astype(jnp.bfloat16)
    placed = jnp.dot(hits, rep, preferred_element_type=jnp.float32)
    bank[...] = jnp.where(taken > 0.5, placed, old.astype(jnp.float32)).astype(jnp.bfloat16)
    def drain(i):
        peer = lax.rem(me + 1 + i, n)
        key_copy(me, peer).wait_send()
        cache_copy(me, peer).wait_send()
        part_copy(me, peer, mine).wait_send()

    each(n - 1, drain)


def relate_kernel(q_v, bank, rel_hbm, bank_hbm, rel_v, sem):
    group, toks, dim = q_v.shape
    local = bank_hbm.shape[0]
    scale = 1.0 / math.sqrt(dim)
    first = pl.multiple_of(lax.axis_index("seq") * local, local)
    keep = pltpu.make_async_copy(bank.at[pl.ds(first, local)], bank_hbm, sem.at[group])
    keep.start()
    outs = [
        pltpu.make_async_copy(rel_v.at[j], rel_hbm.at[j], sem.at[j]) for j in range(group)
    ]
    for j in range(group):
        r = lax.dot_general(q_v[j], bank[...], NT, preferred_element_type=jnp.float32)
        rel_v[j] = (r * scale).astype(jnp.bfloat16)
        outs[j].start()
    for out in outs:
        out.wait()
    keep.wait()


def per_device(n, queries, new_keys, cache_keys, window_start, owner_slot):
    toks, group, dim = queries.shape
    ktoks, local = new_keys.shape[0], cache_keys.shape[0]
    blocks = window_start.shape[0]
    slots = n * local
    hbm_spec = pl.BlockSpec(memory_space=pltpu.HBM)
    vmem_spec = pl.BlockSpec(memory_space=pltpu.VMEM)
    bf16 = jnp.bfloat16
    q_held, bank = pl.pallas_call(
        functools.partial(refresh_kernel, n),
        out_shape=(
            pltpu.VMEM((group, toks, dim), bf16),
            pltpu.VMEM((slots, dim), bf16),
        ),
        in_specs=[hbm_spec] * 5,
        out_specs=(vmem_spec, vmem_spec),
        scratch_shapes=[
            pltpu.SMEM((blocks,), jnp.int32),
            pltpu.VMEM((1, blocks), jnp.int32),
            pltpu.VMEM((dim, group * toks), bf16),
            pltpu.VMEM((n, ktoks, dim), bf16),
            pltpu.VMEM((n, local, dim), bf16),
            pltpu.VMEM((blocks, dim), jnp.float32),
            pltpu.VMEM((n, blocks, dim), jnp.float32),
            pltpu.SemaphoreType.DMA((5,)),
        ] + [pltpu.SemaphoreType.DMA((n,))] * 6,
        compiler_params=pltpu.CompilerParams(
            collective_id=0, has_side_effects=True, vmem_limit_bytes=VMEM - 2 * dim * (group * toks + slots) - 16384
        ),
        name="refresh",
    )(
        window_start,
        owner_slot.reshape(1, blocks),
        jnp.transpose(queries, (1, 0, 2)),
        new_keys.reshape(ktoks, dim),
        cache_keys.reshape(local, dim),
    )
    rel, own = pl.pallas_call(
        relate_kernel,
        out_shape=(
            jax.ShapeDtypeStruct((group, toks, slots), bf16),
            jax.ShapeDtypeStruct((local, dim), bf16),
        ),
        in_specs=[vmem_spec, vmem_spec],
        out_specs=(hbm_spec, hbm_spec),
        scratch_shapes=[
            pltpu.VMEM((group, toks, slots), bf16),
            pltpu.SemaphoreType.DMA((group + 1,)),
        ],
        compiler_params=pltpu.CompilerParams(
            vmem_limit_bytes=2 * group * toks * slots + 16 * 1024 * 1024
        ),
        name="relate",
    )(q_held, bank)
    return jnp.transpose(rel, (1, 0, 2)), own[:, None, :]


def solution(mesh):
    spec = P("seq", "kvh", None)
    return jax.shard_map(
        functools.partial(per_device, mesh.shape["seq"]),
        mesh=mesh,
        in_specs=(spec, spec, spec, P(), P()),
        out_specs=(spec, spec),
        check_vma=False,
    )
```

profile of v0, /device:TPU:0, one launch (start us, length us, event | category | flops | bytes accessed | tf_op | source)
XLA Modules:
  0.0 21.8 jit_solution(12041000983757144145)
XLA Ops:
  0.6 20.0 %refresh.1 = (bf16[7,128,128]{2,1,0:T(8,128)(2,1)S(1)}, bf16[512,128]{1,0:T(8,128)(2,1)S(1)}) custom-call(s32[8]{0:T(128)} %start_hbm.1, s32[1,8]{1,0:T(1,128)} %bitcast.9, bf16[7,128,128]{2,1,0:T(8,128)(2,1)} %bitcast.6, bf16[128,128]{1,0:T(8,128)(2,1)} %bitcast.7, bf16[64,128]{1,0:T(8,128)(2,1)} %bitcast.8), custom_call_target="tpu_custom_call" | custom-call | tf_op jit(solution)/shard_map/refresh/pallas_call | solution.py:175
  20.6 1.2 %relate.1 = (bf16[7,128,512]{2,1,0:T(8,128)(2,1)}, bf16[64,128]{1,0:T(8,128)(2,1)}) custom-call(bf16[7,128,128]{2,1,0:T(8,128)(2,1)S(1)} %get-tuple-element.6.q_v, bf16[512,128]{1,0:T(8,128)(2,1)S(1)} %get-tuple-element.7.bank), custom_call_target="tpu_custom_call" | custom-call | tf_op jit(solution)/shard_map/relate/pallas_call | solution.py:204
where the time goes:
time: 21.9 us; the launch traced here: 21.8 us
  Pallas kernels  21.2 us (97%)
  between operations  0.64 us (3%)
    pallas_call x1, Pallas kernels, per_device(): pl.pallas_call(functools.partial(refresh_kernel, n), out_shape=(pltpu.VME...  20 us
    pallas_call x1, Pallas kernels, per_device(): pl.pallas_call(relate_kernel, out_shape=(jax.ShapeDtypeStruct((group, tok...  1.19 us

commit v1 on v0

--- a/solution.py
+++ b/solution.py
@@ -145,6 +145,269 @@
     each(n - 1, drain)
 
 
+def line_kernel(
+    n, start_hbm, slot_hbm, q_hbm, k_hbm, c_hbm, q_v, bank,
+    start_ref, slot_ref, q_t, keys, cache, mine, parts,
+    load_sem, ready, ks_sem, kf_sem, kr_sem, cs_sem, cf_sem, cr_sem, ps_sem, pr_sem,
+):
+    group, toks, dim = q_v.shape
+    ktoks = keys.shape[1]
+    local = cache.shape[1]
+    slots = n * local
+    per = ktoks // BLK
+    blocks = n * per
+    rows = n // 2
+    scale = 1.0 / math.sqrt(dim)
+    me = lax.axis_index("seq")
+    row = me // 2
+    side = me % 2
+    pair = me + 1 - 2 * side
+
+    load_k = pltpu.make_async_copy(k_hbm, keys.at[me], load_sem.at[0])
+    load_q = pltpu.make_async_copy(q_hbm, q_v, load_sem.at[1])
+    load_c = pltpu.make_async_copy(c_hbm, cache.at[me], load_sem.at[2])
+    load_w = pltpu.make_async_copy(start_hbm, start_ref, load_sem.at[3])
+    load_s = pltpu.make_async_copy(slot_hbm, slot_ref, load_sem.at[4])
+    load_k.start()
+    load_q.start()
+    load_c.start()
+    load_w.start()
+    load_s.start()
+
+    barrier = pltpu.get_barrier_semaphore()
+
+    def signal(sem, peer):
+        pl.semaphore_signal(
+            sem, inc=1, device_id={"seq": peer}, device_id_type=pl.DeviceIdType.MESH
+        )
+
+    def mate(other):
+        return 2 * other + side
+
+    @pl.when(side == 0)
+    def _():
+        signal(barrier, pair)
+
+    for other in range(1, rows):
+        @pl.when(other > row)
+        def _(other=other):
+            signal(barrier, mate(other))
+
+        @pl.when((other > row) & (side == 0))
+        def _(other=other):
+            signal(barrier, mate(other) + 1)
+
+    @pl.when(me > 0)
+    def _():
+        pl.semaphore_wait(barrier, row + side * (row + 1))
+
+    @pl.when(side == 1)
+    def _():
+        signal(ready.at[me], pair)
+
+    for other in reversed(range(rows - 1)):
+        @pl.when(other < row)
+        def _(other=other):
+            signal(ready.at[me], mate(other))
+
+        @pl.when((other < row) & (side == 1))
+        def _(other=other):
+            signal(ready.at[me], mate(other) - 1)
+
+    def link(src, dst, s_sem, r_sem, peer):
+        return pltpu.make_async_remote_copy(
+            src_ref=src, dst_ref=dst, send_sem=s_sem, recv_sem=r_sem,
+            device_id={"seq": peer}, device_id_type=pl.DeviceIdType.MESH,
+        )
+
+    def key_copy(slot, peer, sem):
+        return link(keys.at[slot], keys.at[slot], sem, kr_sem.at[slot], peer)
+
+    def cache_copy(slot, peer, sem):
+        return link(cache.at[slot], cache.at[slot], sem, cr_sem.at[slot], peer)
+
+    def part_copy(slot, peer, src):
+        return link(src, parts.at[slot], ps_sem.at[peer], pr_sem.at[slot], peer)
+
+    def own_key(peer):
+        return key_copy(me, peer, ks_sem.at[peer])
+
+    def own_cache(peer):
+        return cache_copy(me, peer, cs_sem.at[peer])
+
+    def partial(owner):
+        for p in range(per):
+            index = owner * per + p
+            kb = keys[owner, p * BLK:(p + 1) * BLK, :]
+            begin = start_ref[index]
+            mask = jnp.where((position >= begin) & (position < begin + WIN), 1.0, 0.0)
+            s = jnp.dot(kb, q_t[...], preferred_element_type=jnp.float32)
+            top = jnp.max(s, axis=0, keepdims=True)
+            e = jnp.exp2((s - top) * (scale * LOG2E))
+            total = jnp.sum(e, axis=0, keepdims=True)
+            acc = None
+            for j in range(group):
+                cols = slice(j * toks, (j + 1) * toks)
+                term = e[:, cols] * (mask / total[:, cols])
+                acc = term if acc is None else acc + term
+            weight = jnp.sum(acc, axis=1, keepdims=True)
+            rep = jnp.sum(weight * kb.astype(jnp.float32), axis=0, keepdims=True)
+            mine[pl.ds(index, 1), :] = rep
+
+    load_k.wait()
+
+    @pl.when(side == 1)
+    def _():
+        own_key(pair).start()
+
+    for dist in range(1, rows):
+        @pl.when(row - dist >= 0)
+        def _(dist=dist):
+            own_key(me - 2 * dist).start()
+
+        if dist in ():
+            @pl.when((row - dist >= 0) & (side == 1))
+            def _(dist=dist):
+                own_key(me - 2 * dist - 1).start()
+
+    def later(dist):
+        @pl.when(row + dist < rows)
+        def _():
+            peer = me + 2 * dist
+            pl.semaphore_wait(ready.at[peer], 1)
+            own_key(peer).start()
+
+        @pl.when((row + dist < rows) & (side == 0))
+        def _():
+            pl.semaphore_wait(ready.at[me + 2 * dist + 1], 1)
+
+        if dist in ():
+            @pl.when(row + dist < rows)
+            def _():
+                own_key(me + 2 * dist + 1 - 2 * side).start()
+
+    @pl.when(side == 0)
+    def _():
+        pl.semaphore_wait(ready.at[pair], 1)
+        own_key(pair).start()
+
+    for dist in ():
+        @pl.when((row - dist >= 0) & (side == 0))
+        def _(dist=dist):
+            own_key(me - 2 * dist + 1).start()
+
+    later(1)
+
+    load_q.wait()
+    load_w.wait()
+    load_s.wait()
+    for j in range(group):
+        q_t[:, j * toks:(j + 1) * toks] = q_v[j].T
+    position = me * toks + lax.broadcasted_iota(jnp.int32, (1, toks), 1)
+    later(2)
+    partial(me)
+    for dist in range(3, rows):
+        later(dist)
+
+    def pick(values):
+        out = values[0]
+        for r in range(1, rows):
+            if values[r] != values[0]:
+                out = jnp.where(row == r, values[r], out)
+        return out
+
+    near = [sorted((r for r in range(rows) if r != z), key=lambda r: (abs(r - z), r)) for z in range(rows)]
+    def due(z, other, cross):
+        dist = abs(z - other)
+        when = 5.0 + 0.5 * dist
+        if cross and dist not in ():
+            return when + 3.6
+        return when + (1.0 if cross else 0)
+
+    order = [
+        sorted((due(z, r, c), r, c, int(c == 0 and abs(r - z) not in ())) for r in near[z] for c in (0, 1))
+        for z in range(rows)
+    ]
+
+    def fwd_key(owner):
+        return key_copy(owner, pair, kf_sem.at[owner])
+
+    def fwd_cache(owner):
+        return cache_copy(owner, pair, cf_sem.at[owner])
+
+    def chosen(step):
+        z, cross, fwd = (pick([order[r][step][i] for r in range(rows)]) for i in (1, 2, 3))
+        return 2 * z + side + cross * (1 - 2 * side), fwd
+
+    def own_caches(act):
+        act(own_cache(pair))
+        for dist in range(1, rows):
+            for peer, there in ((me + 2 * dist, row + dist < rows), (me - 2 * dist, row - dist >= 0)):
+                @pl.when(there)
+                def _(peer=peer):
+                    act(own_cache(peer))
+
+    key_copy(pair, pair, ks_sem.at[pair]).wait_recv()
+    partial(pair)
+    for step in range(len(order[0])):
+        owner, fwd = chosen(step)
+        key_copy(owner, owner, ks_sem.at[owner]).wait_recv()
+        if isinstance(fwd, int):
+            if fwd:
+                fwd_key(owner).start()
+        else:
+            @pl.when(fwd == 1)
+            def _(owner=owner):
+                fwd_key(owner).start()
+        if step == 2:
+            load_c.wait()
+            own_caches(lambda copy: copy.start())
+        partial(owner)
+
+    each(n - 1, lambda i: part_copy(me, lax.rem(me + 1 + i, n), mine).start())
+
+    lines = [pick([near[z][i] for z in range(rows)]) for i in range(rows - 1)]
+    for z in lines:
+        owner = 2 * z + side
+        cache_copy(owner, owner, cs_sem.at[owner]).wait_recv()
+        fwd_cache(owner).start()
+    cache_copy(pair, pair, cs_sem.at[pair]).wait_recv()
+    for z in lines:
+        owner = 2 * z + 1 - side
+        cache_copy(owner, owner, cs_sem.at[owner]).wait_recv()
+    hits = jnp.where(
+        lax.broadcasted_iota(jnp.int32, (slots, blocks), 0) == slot_ref[...], 1.0, 0.0
+    )
+    taken = jnp.max(hits, axis=1, keepdims=True)
+    hits = hits.astype(jnp.bfloat16)
+    old = cache[...].reshape(slots, dim)
+
+    each(n - 1, lambda i: part_copy(lax.rem(me + n - 1 - i, n), me, mine).wait_recv())
+    parts[me] = mine[...]
+    rep_sum = parts[0]
+    for d in range(1, n):
+        rep_sum = rep_sum + parts[d]
+    rep = (rep_sum * (1.0 / (group * WIN))).astype(jnp.bfloat16)
+    placed = jnp.dot(hits, rep, preferred_element_type=jnp.float32)
+    bank[...] = jnp.where(taken > 0.5, placed, old.astype(jnp.float32)).astype(jnp.bfloat16)
+
+    own_caches(lambda copy: copy.wait_send())
+    own_key(pair).wait_send()
+    for z in lines:
+        owner = 2 * z + side
+        own_key(owner).wait_send()
+        fwd_cache(owner).wait_send()
+    for dist in range(1, rows):
+        for peer, there in ((me + 2 * dist, row + dist < rows), (me - 2 * dist, row - dist >= 0)):
+            @pl.when(there)
+            def _(peer=peer, dist=dist):
+                if dist in ():
+                    own_key(peer + 1 - 2 * side).wait_send()
+                else:
+                    fwd_key(peer).wait_send()
+    each(n - 1, lambda i: part_copy(me, lax.rem(me + 1 + i, n), mine).wait_send())
+
+
 def relate_kernel(q_v, bank, rel_hbm, bank_hbm, rel_v, sem):
     group, toks, dim = q_v.shape
     local = bank_hbm.shape[0]
@@ -172,8 +435,12 @@
     hbm_spec = pl.BlockSpec(memory_space=pltpu.HBM)
     vmem_spec = pl.BlockSpec(memory_space=pltpu.VMEM)
     bf16 = jnp.bfloat16
+    short = n % 2 == 0 and n <= 8
+    sems = [pltpu.SemaphoreType.DMA((n,))] * (8 if short else 6)
+    if short:
+        sems = [pltpu.SemaphoreType.REGULAR((n,))] + sems
     q_held, bank = pl.pallas_call(
-        functools.partial(refresh_kernel, n),
+        functools.partial(line_kernel if short else refresh_kernel, n),
         out_shape=(
             pltpu.VMEM((group, toks, dim), bf16),
             pltpu.VMEM((slots, dim), bf16),
@@ -189,7 +456,7 @@
             pltpu.VMEM((blocks, dim), jnp.float32),
             pltpu.VMEM((n, blocks, dim), jnp.float32),
             pltpu.SemaphoreType.DMA((5,)),
-        ] + [pltpu.SemaphoreType.DMA((n,))] * 6,
+        ] + sems,
         compiler_params=pltpu.CompilerParams(
             collective_id=0, has_side_effects=True, vmem_limit_bytes=VMEM - 2 * dim * (group * toks + slots) - 16384
         ),

time: 21.9 us -> 20.2 us (0.922)
  Pallas kernels: 21.2 us -> 19.4 us
    pallas_call x1, Pallas kernels: 20 us -> 18.2 us  [per_device(): pl.pallas_call(functools.partial(line_kernel if short else refresh_kernel...]
where the time goes in v1:
time: 20.2 us; the launch traced here: 20 us
  Pallas kernels  19.4 us (96%)
  between operations  0.64 us (3%)
    pallas_call x1, Pallas kernels, per_device(): pl.pallas_call(functools.partial(line_kernel if short else refresh_kernel...  18.2 us
    pallas_call x1, Pallas kernels, per_device(): pl.pallas_call(relate_kernel, out_shape=(jax.ShapeDtypeStruct((group, tok...  1.19 us

profile of v1, /device:TPU:0, one launch (start us, length us, event | category | flops | bytes accessed | tf_op | source)
XLA Modules:
  0.0 20.0 jit_solution(7612343864318827811)
XLA Ops:
  0.6 18.2 %refresh.1 = (bf16[7,128,128]{2,1,0:T(8,128)(2,1)S(1)}, bf16[512,128]{1,0:T(8,128)(2,1)S(1)}) custom-call(s32[8]{0:T(128)} %start_hbm.1, s32[1,8]{1,0:T(1,128)} %bitcast.9, bf16[7,128,128]{2,1,0:T(8,128)(2,1)} %bitcast.6, bf16[128,128]{1,0:T(8,128)(2,1)} %bitcast.7, bf16[64,128]{1,0:T(8,128)(2,1)} %bitcast.8), custom_call_target="tpu_custom_call" | custom-call | tf_op jit(solution)/shard_map/refresh/pallas_call | solution.py:442
  18.8 1.2 %relate.1 = (bf16[7,128,512]{2,1,0:T(8,128)(2,1)}, bf16[64,128]{1,0:T(8,128)(2,1)}) custom-call(bf16[7,128,128]{2,1,0:T(8,128)(2,1)S(1)} %get-tuple-element.6.q_v, bf16[512,128]{1,0:T(8,128)(2,1)S(1)} %get-tuple-element.7.bank), custom_call_target="tpu_custom_call" | custom-call | tf_op jit(solution)/shard_map/relate/pallas_call | solution.py:471

commit v2 on v0

--- a/solution.py
+++ b/solution.py
@@ -145,6 +145,294 @@
     each(n - 1, drain)
 
 
+FAR = [3, 9]
+CHAIN = [0, 0]
+UP_AT = [1, 1]
+DOWN_AT = [5, 5]
+PAIR_AT = [3, 3]
+HAND_UP = [4, 5, 6]
+HAND_DOWN = [7, 7, 7]
+T_PAIR = [5.0, 3.9]
+T_LINE = [4.9, 4.0]
+T_HOP = [0.9, 2.2]
+T_RELAY = [3.2, 2.2]
+T_FAR = [7.0, 9.0]
+
+
+def plan(rows, group):
+    far, chain = FAR[group], CHAIN[group]
+    table = []
+    for z in range(rows):
+        blocks = [(T_PAIR[group], z, 1, 0, tuple(r for r in range(rows) if r - z >= far))]
+        for r in range(rows):
+            if r == z:
+                continue
+            line = T_LINE[group] + T_HOP[group] * (abs(r - z) - 1)
+            on = z + (1 if z > r else -1)
+            blocks.append((line, r, 0, int(z - r < far), (on,) if chain and 0 <= on < rows else ()))
+            blocks.append((T_FAR[group] if z - r >= far else line + T_RELAY[group], r, 1, 0, ()))
+        table.append([b[1:] for b in sorted(blocks)])
+    return table
+
+
+def line_kernel(
+    n, start_hbm, slot_hbm, q_hbm, k_hbm, c_hbm, q_v, bank,
+    start_ref, slot_ref, q_t, keys, cache, mine, parts,
+    load_sem, ready, ks_sem, kf_sem, kl_sem, kr_sem, cs_sem, cf_sem, cr_sem, ps_sem, pr_sem,
+):
+    group, toks, dim = q_v.shape
+    ktoks = keys.shape[1]
+    local = cache.shape[1]
+    slots = n * local
+    per = ktoks // BLK
+    blocks = n * per
+    rows = n // 2
+    scale = 1.0 / math.sqrt(dim)
+    me = lax.axis_index("seq")
+    second = lax.axis_index("kvh") % 2
+    row = me // 2
+    side = me % 2
+    pair = me + 1 - 2 * side
+
+    load_k = pltpu.make_async_copy(k_hbm, keys.at[me], load_sem.at[0])
+    load_q = pltpu.make_async_copy(q_hbm, q_v, load_sem.at[1])
+    load_c = pltpu.make_async_copy(c_hbm, cache.at[me], load_sem.at[2])
+    load_w = pltpu.make_async_copy(start_hbm, start_ref, load_sem.at[3])
+    load_s = pltpu.make_async_copy(slot_hbm, slot_ref, load_sem.at[4])
+    load_k.start()
+    load_q.start()
+    load_c.start()
+    load_w.start()
+    load_s.start()
+
+    barrier = pltpu.get_barrier_semaphore()
+
+    def signal(sem, peer):
+        pl.semaphore_signal(
+            sem, inc=1, device_id={"seq": peer}, device_id_type=pl.DeviceIdType.MESH
+        )
+
+    def when(flag, act):
+        if isinstance(flag, (bool, int)):
+            if flag:
+                act()
+        else:
+            pl.when(flag)(act)
+
+    def mate(other):
+        return 2 * other + side
+
+    when(side == 0, lambda: signal(barrier, pair))
+    for other in range(1, rows):
+        when(other > row, lambda: signal(barrier, mate(other)))
+
+    when(me > 0, lambda: pl.semaphore_wait(barrier, row + side))
+    when(side == 1, lambda: signal(ready.at[me], pair))
+    for other in reversed(range(rows - 1)):
+        when(other < row, lambda: signal(ready.at[me], mate(other)))
+
+    def link(src, dst, s_sem, r_sem, peer):
+        return pltpu.make_async_remote_copy(
+            src_ref=src, dst_ref=dst, send_sem=s_sem, recv_sem=r_sem,
+            device_id={"seq": peer}, device_id_type=pl.DeviceIdType.MESH,
+        )
+
+    def key_copy(slot, peer, sem):
+        return link(keys.at[slot], keys.at[slot], sem, kr_sem.at[slot], peer)
+
+    def cache_copy(slot, peer, sem):
+        return link(cache.at[slot], cache.at[slot], sem, cr_sem.at[slot], peer)
+
+    def part_copy(slot, peer, src):
+        return link(src, parts.at[slot], ps_sem.at[peer], pr_sem.at[slot], peer)
+
+    def own_key(peer):
+        return key_copy(me, peer, ks_sem.at[peer])
+
+    def own_cache(peer):
+        return cache_copy(me, peer, cs_sem.at[peer])
+
+    def hand_key(owner):
+        return key_copy(owner, pair, kf_sem.at[owner])
+
+    def pass_key(owner, other):
+        return key_copy(owner, mate(other), kl_sem.at[owner * rows + other])
+
+    def hand_cache(owner):
+        return cache_copy(owner, pair, cf_sem.at[owner])
+
+    def pick(values):
+        flat = [v for group in values for v in group]
+        if len(set(flat)) == 1:
+            return flat[0]
+        out = flat[0]
+        for at, v in enumerate(flat):
+            if v != flat[0]:
+                out = jnp.where(second * rows + row == at, v, out)
+        return out
+
+    tables = [plan(rows, g) for g in range(2)]
+
+    def block(step):
+        z, cross, to_pair = (
+            pick([[t[r][step][i] for r in range(rows)] for t in tables]) for i in range(3)
+        )
+        onward = [
+            (other, pick([[int(other in t[r][step][3]) for r in range(rows)] for t in tables]))
+            for other in range(rows)
+        ]
+        return mate(z) + cross * (1 - 2 * side), to_pair, onward
+
+    def flag(value):
+        return bool(value) if isinstance(value, int) else value == 1
+
+    def relays(step, act):
+        owner, to_pair, onward = block(step)
+        when(flag(to_pair), lambda: act(hand_key(owner)))
+        for other, there in onward:
+            when(flag(there), lambda: act(pass_key(owner, other)))
+
+    def line_key(dist, act):
+        there = (0 <= row + dist) & (row + dist < rows)
+        straight = [abs(dist) == 1 or not chain for chain in CHAIN]
+        if not all(straight):
+            there = there & (second == straight.index(True)) if any(straight) else False
+        when(there, lambda: act(own_key(me + 2 * dist)))
+
+    def up_caches(act):
+        for dist in range(1, rows):
+            when(row - dist >= 0, lambda: act(own_cache(me - 2 * dist)))
+
+    def down_caches(act):
+        for dist in range(1, rows):
+            when(row + dist < rows, lambda: act(own_cache(me + 2 * dist)))
+
+    def at_step(places, step, act):
+        if all(p == step for p in places):
+            act()
+        else:
+            for g, p in enumerate(places):
+                if p == step:
+                    when(second == g, act)
+
+    lines = [
+        pick([[sorted((abs(r - z), r) for r in range(rows) if r != z)[i][1] for z in range(rows)]] * 2)
+        for i in range(rows - 1)
+    ]
+
+    def caches(step):
+        at_step(UP_AT, step, lambda: up_caches(lambda copy: copy.start()))
+        at_step(DOWN_AT, step, lambda: down_caches(lambda copy: copy.start()))
+        at_step(PAIR_AT, step, lambda: own_cache(pair).start())
+
+        def hand(peer):
+            cache_copy(peer, peer, cs_sem.at[peer]).wait_recv()
+            hand_cache(peer).start()
+
+        for dist in range(1, rows):
+            if HAND_UP[dist - 1] == step:
+                when(row + dist < rows, lambda: hand(me + 2 * dist))
+            if HAND_DOWN[dist - 1] == step:
+                when(row - dist >= 0, lambda: hand(me - 2 * dist))
+
+    def partial(owner):
+        for p in range(per):
+            index = owner * per + p
+            kb = keys[owner, p * BLK:(p + 1) * BLK, :]
+            begin = start_ref[index]
+            mask = jnp.where((position >= begin) & (position < begin + WIN), 1.0, 0.0)
+            s = jnp.dot(kb, q_t[...], preferred_element_type=jnp.float32)
+            top = jnp.max(s, axis=0, keepdims=True)
+            e = jnp.exp2((s - top) * (scale * LOG2E))
+            total = jnp.sum(e, axis=0, keepdims=True)
+            acc = None
+            for j in range(group):
+                cols = slice(j * toks, (j + 1) * toks)
+                term = e[:, cols] * (mask / total[:, cols])
+                acc = term if acc is None else acc + term
+            weight = jnp.sum(acc, axis=1, keepdims=True)
+            rep = jnp.sum(weight * kb.astype(jnp.float32), axis=0, keepdims=True)
+            mine[pl.ds(index, 1), :] = rep
+
+    load_k.wait()
+
+    when(side == 1, lambda: own_key(pair).start())
+    for dist in range(1, rows):
+        line_key(-dist, lambda copy: copy.start())
+
+    def later(dist):
+        when(row + dist < rows, lambda: pl.semaphore_wait(ready.at[me + 2 * dist], 1))
+        line_key(dist, lambda copy: copy.start())
+
+    def to_pair():
+        pl.semaphore_wait(ready.at[pair], 1)
+        own_key(pair).start()
+
+    when(side == 0, to_pair)
+    later(1)
+    load_q.wait()
+    load_w.wait()
+    load_s.wait()
+    for j in range(group):
+        q_t[:, j * toks:(j + 1) * toks] = q_v[j].T
+    position = me * toks + lax.broadcasted_iota(jnp.int32, (1, toks), 1)
+    later(2)
+    partial(me)
+    for dist in range(3, rows):
+        later(dist)
+    load_c.wait()
+    caches(-1)
+
+    done = 0
+    for step in range(n - 1):
+        owner = block(step)[0]
+        key_copy(owner, owner, ks_sem.at[owner]).wait_recv()
+        relays(step, lambda copy: copy.start())
+        caches(step)
+        if step >= 2 - 1:
+            for at in range(done, step + 1):
+                partial(block(at)[0])
+            done = step + 1
+
+    each(n - 1, lambda i: part_copy(me, lax.rem(me + 1 + i, n), mine).start())
+    caches(n - 1)
+    cache_copy(pair, pair, cs_sem.at[pair]).wait_recv()
+    for z in lines:
+        owner = mate(z) + 1 - 2 * side
+        cache_copy(owner, owner, cs_sem.at[owner]).wait_recv()
+    hits = jnp.where(
+        lax.broadcasted_iota(jnp.int32, (slots, blocks), 0) == slot_ref[...], 1.0, 0.0
+    )
+    taken = jnp.max(hits, axis=1, keepdims=True)
+    hits = hits.astype(jnp.bfloat16)
+    old = cache[...].reshape(slots, dim)
+
+    each(n - 1, lambda i: part_copy(lax.rem(me + n - 1 - i, n), me, mine).wait_recv())
+    parts[me] = mine[...]
+    rep_sum = parts[0]
+    for d in range(1, n):
+        rep_sum = rep_sum + parts[d]
+    rep = (rep_sum * (1.0 / (group * WIN))).astype(jnp.bfloat16)
+    placed = jnp.dot(hits, rep, preferred_element_type=jnp.float32)
+    bank[...] = jnp.where(taken > 0.5, placed, old.astype(jnp.float32)).astype(jnp.bfloat16)
+
+    def sent(copy):
+        copy.wait_send()
+
+    sent(own_key(pair))
+    sent(own_cache(pair))
+    up_caches(sent)
+    down_caches(sent)
+    for dist in range(1, rows):
+        line_key(-dist, sent)
+        line_key(dist, sent)
+    for z in lines:
+        sent(hand_cache(mate(z)))
+    for step in range(n - 1):
+        relays(step, sent)
+    each(n - 1, lambda i: sent(part_copy(me, lax.rem(me + 1 + i, n), mine)))
+
+
 def relate_kernel(q_v, bank, rel_hbm, bank_hbm, rel_v, sem):
     group, toks, dim = q_v.shape
     local = bank_hbm.shape[0]
@@ -172,8 +460,17 @@
     hbm_spec = pl.BlockSpec(memory_space=pltpu.HBM)
     vmem_spec = pl.BlockSpec(memory_space=pltpu.VMEM)
     bf16 = jnp.bfloat16
+    short = n % 2 == 0 and n <= 8
+    sems = [pltpu.SemaphoreType.DMA((n,))] * 6
+    if short:
+        sems = (
+            [pltpu.SemaphoreType.REGULAR((n,))]
+            + [pltpu.SemaphoreType.DMA((n,))] * 2
+            + [pltpu.SemaphoreType.DMA((n * n // 2,))]
+            + [pltpu.SemaphoreType.DMA((n,))] * 6
+        )
     q_held, bank = pl.pallas_call(
-        functools.partial(refresh_kernel, n),
+        functools.partial(line_kernel if short else refresh_kernel, n),
         out_shape=(
             pltpu.VMEM((group, toks, dim), bf16),
             pltpu.VMEM((slots, dim), bf16),
@@ -189,7 +486,7 @@
             pltpu.VMEM((blocks, dim), jnp.float32),
             pltpu.VMEM((n, blocks, dim), jnp.float32),
             pltpu.SemaphoreType.DMA((5,)),
-        ] + [pltpu.SemaphoreType.DMA((n,))] * 6,
+        ] + sems,
         compiler_params=pltpu.CompilerParams(
             collective_id=0, has_side_effects=True, vmem_limit_bytes=VMEM - 2 * dim * (group * toks + slots) - 16384
         ),

time: 21.9 us -> 19.4 us (0.89)
  Pallas kernels: 21.2 us -> 18.6 us
    pallas_call x1, Pallas kernels: 20 us -> 17.4 us  [per_device(): pl.pallas_call(functools.partial(line_kernel if short else refresh_kernel...]
where the time goes in v2:
time: 19.4 us; the launch traced here: 19.3 us
  Pallas kernels  18.6 us (96%)
  between operations  0.64 us (3%)
    pallas_call x1, Pallas kernels, per_device(): pl.pallas_call(functools.partial(line_kernel if short else refresh_kernel...  17.4 us
    pallas_call x1, Pallas kernels, per_device(): pl.pallas_call(relate_kernel, out_shape=(jax.ShapeDtypeStruct((group, tok...  1.19 us

profile of v2, /device:TPU:0, one launch (start us, length us, event | category | flops | bytes accessed | tf_op | source)
XLA Modules:
  0.0 19.3 jit_solution(14761485187721643015)
XLA Ops:
  0.6 17.4 %refresh.1 = (bf16[7,128,128]{2,1,0:T(8,128)(2,1)S(1)}, bf16[512,128]{1,0:T(8,128)(2,1)S(1)}) custom-call(s32[8]{0:T(128)} %start_hbm.1, s32[1,8]{1,0:T(1,128)} %bitcast.9, bf16[7,128,128]{2,1,0:T(8,128)(2,1)} %bitcast.6, bf16[128,128]{1,0:T(8,128)(2,1)} %bitcast.7, bf16[64,128]{1,0:T(8,128)(2,1)} %bitcast.8), custom_call_target="tpu_custom_call" | custom-call | tf_op jit(solution)/shard_map/refresh/pallas_call | solution.py:472
  18.1 1.2 %relate.1 = (bf16[7,128,512]{2,1,0:T(8,128)(2,1)}, bf16[64,128]{1,0:T(8,128)(2,1)}) custom-call(bf16[7,128,128]{2,1,0:T(8,128)(2,1)S(1)} %get-tuple-element.6.q_v, bf16[512,128]{1,0:T(8,128)(2,1)S(1)} %get-tuple-element.7.bank), custom_call_target="tpu_custom_call" | custom-call | tf_op jit(solution)/shard_map/relate/pallas_call | solution.py:501

commit v3 on v2

--- a/solution.py
+++ b/solution.py
@@ -145,14 +145,18 @@
     each(n - 1, drain)
 
 
-FAR = [3, 9]
+FAR = [2, 9]
+UP = [(3,), ()]
+CUP = [(1, 2, 3), ()]
+DOWN = [(), ()]
+T_DIAG = [0.8, 0.8]
 CHAIN = [0, 0]
-UP_AT = [1, 1]
-DOWN_AT = [5, 5]
+UP_AT = [2, 2]
+DOWN_AT = [4, 4]
 PAIR_AT = [3, 3]
-HAND_UP = [4, 5, 6]
+HAND_UP = [7, 7, 7]
 HAND_DOWN = [7, 7, 7]
-T_PAIR = [5.0, 3.9]
+T_PAIR = [4.0, 3.9]
 T_LINE = [4.9, 4.0]
 T_HOP = [0.9, 2.2]
 T_RELAY = [3.2, 2.2]
@@ -162,15 +166,21 @@
 def plan(rows, group):
     far, chain = FAR[group], CHAIN[group]
     table = []
+
+    def swaps(a, b):
+        return b - a >= far and (b == rows - 1 or not 1)
+
     for z in range(rows):
-        blocks = [(T_PAIR[group], z, 1, 0, tuple(r for r in range(rows) if r - z >= far))]
+        blocks = [(T_PAIR[group], z, 1, 0, tuple(r for r in range(rows) if swaps(z, r)))]
         for r in range(rows):
             if r == z:
                 continue
             line = T_LINE[group] + T_HOP[group] * (abs(r - z) - 1)
             on = z + (1 if z > r else -1)
-            blocks.append((line, r, 0, int(z - r < far), (on,) if chain and 0 <= on < rows else ()))
-            blocks.append((T_FAR[group] if z - r >= far else line + T_RELAY[group], r, 1, 0, ()))
+            straight = abs(r - z) in (DOWN if r < z else UP)[group] and (r > z or z == rows - 1 or not 0)
+            blocks.append((line, r, 0, int(not swaps(r, z) and not straight), (on,) if chain and 0 <= on < rows else ()))
+            other = line + (T_DIAG if straight else T_RELAY)[group]
+            blocks.append((T_FAR[group] if swaps(r, z) else other, r, 1, 0, ()))
         table.append([b[1:] for b in sorted(blocks)])
     return table
 
@@ -226,10 +236,29 @@
     for other in range(1, rows):
         when(other > row, lambda: signal(barrier, mate(other)))
 
-    when(me > 0, lambda: pl.semaphore_wait(barrier, row + side))
+    def diagonal(sets, dist, there, act):
+        there = (0 <= row + dist) & (row + dist < rows) & there
+        if 0 and sets is DOWN:
+            there = there & ((row == rows - 1) if dist < 0 else (row + dist == rows - 1))
+        has = [abs(dist) in g for g in sets]
+        if any(has):
+            when(there if all(has) else there & (second == has.index(True)), act)
+
+    both = [set(a) | set(b) | set(c) for a, b, c in zip(UP, DOWN, CUP)]
+    for dist in range(1, rows):
+        diagonal(both, dist, side == 0, lambda: signal(barrier, me + 2 * dist + 1))
+
+    count = row + side
+    for g in range(2):
+        for dist in sorted(both[g]):
+            count = count + jnp.where((side == 1) & (row >= dist) & (second == g), 1, 0)
+
+    when(me > 0, lambda: pl.semaphore_wait(barrier, count))
     when(side == 1, lambda: signal(ready.at[me], pair))
     for other in reversed(range(rows - 1)):
         when(other < row, lambda: signal(ready.at[me], mate(other)))
+    for dist in reversed(range(1, rows)):
+        diagonal(DOWN, -dist, side == 1, lambda: signal(ready.at[me], me - 2 * dist - 1))
 
     def link(src, dst, s_sem, r_sem, peer):
         return pltpu.make_async_remote_copy(
@@ -302,6 +331,7 @@
     def up_caches(act):
         for dist in range(1, rows):
             when(row - dist >= 0, lambda: act(own_cache(me - 2 * dist)))
+            diagonal(CUP, -dist, True, lambda: act(own_cache(me - 2 * dist + 1 - 2 * side)))
 
     def down_caches(act):
         for dist in range(1, rows):
@@ -320,18 +350,26 @@
         for i in range(rows - 1)
     ]
 
+    def handing(dist, act, other):
+        there = row + dist < rows
+        for g in range(2):
+            when(there & (second == g), other if dist in CUP[g] else act)
+
     def caches(step):
         at_step(UP_AT, step, lambda: up_caches(lambda copy: copy.start()))
         at_step(DOWN_AT, step, lambda: down_caches(lambda copy: copy.start()))
         at_step(PAIR_AT, step, lambda: own_cache(pair).start())
 
+        def here(peer):
+            cache_copy(peer, peer, cs_sem.at[peer]).wait_recv()
+
         def hand(peer):
-            cache_copy(peer, peer, cs_sem.at[peer]).wait_recv()
+            here(peer)
             hand_cache(peer).start()
 
         for dist in range(1, rows):
             if HAND_UP[dist - 1] == step:
-                when(row + dist < rows, lambda: hand(me + 2 * dist))
+                handing(dist, lambda: hand(me + 2 * dist), lambda: here(me + 2 * dist))
             if HAND_DOWN[dist - 1] == step:
                 when(row - dist >= 0, lambda: hand(me - 2 * dist))
 
@@ -357,18 +395,24 @@
     load_k.wait()
 
     when(side == 1, lambda: own_key(pair).start())
+    for dist in reversed(range(1, rows)):
+        line_key(-dist, lambda copy: copy.start())
     for dist in range(1, rows):
-        line_key(-dist, lambda copy: copy.start())
+        diagonal(UP, -dist, side == 1, lambda: own_key(me - 2 * dist - 1).start())
 
     def later(dist):
         when(row + dist < rows, lambda: pl.semaphore_wait(ready.at[me + 2 * dist], 1))
         line_key(dist, lambda copy: copy.start())
+        diagonal(DOWN, dist, side == 0, lambda: pl.semaphore_wait(ready.at[me + 2 * dist + 1], 1))
+        diagonal(DOWN, dist, True, lambda: own_key(me + 2 * dist + 1 - 2 * side).start())
 
     def to_pair():
         pl.semaphore_wait(ready.at[pair], 1)
         own_key(pair).start()
 
     when(side == 0, to_pair)
+    for dist in range(1, rows):
+        diagonal(UP, -dist, side == 0, lambda: own_key(me - 2 * dist + 1).start())
     later(1)
     load_q.wait()
     load_w.wait()
@@ -389,13 +433,14 @@
         key_copy(owner, owner, ks_sem.at[owner]).wait_recv()
         relays(step, lambda copy: copy.start())
         caches(step)
-        if step >= 2 - 1:
+        if step >= 3 - 1:
             for at in range(done, step + 1):
                 partial(block(at)[0])
             done = step + 1
 
-    each(n - 1, lambda i: part_copy(me, lax.rem(me + 1 + i, n), mine).start())
+    each(n - 1, lambda i: part_copy(me, i + jnp.where(i >= me, 1, 0), mine).start())
     caches(n - 1)
+    caches(n)
     cache_copy(pair, pair, cs_sem.at[pair]).wait_recv()
     for z in lines:
         owner = mate(z) + 1 - 2 * side
@@ -424,13 +469,15 @@
     up_caches(sent)
     down_caches(sent)
     for dist in range(1, rows):
-        line_key(-dist, sent)
-        line_key(dist, sent)
-    for z in lines:
-        sent(hand_cache(mate(z)))
+        for to, sets in ((-dist, UP), (dist, DOWN)):
+            line_key(to, sent)
+            diagonal(sets, to, True, lambda: sent(own_key(me + 2 * to + 1 - 2 * side)))
+    for dist in range(1, rows):
+        when(row - dist >= 0, lambda: sent(hand_cache(me - 2 * dist)))
+        handing(dist, lambda: sent(hand_cache(me + 2 * dist)), lambda: None)
     for step in range(n - 1):
         relays(step, sent)
-    each(n - 1, lambda i: sent(part_copy(me, lax.rem(me + 1 + i, n), mine)))
+    each(n - 1, lambda i: sent(part_copy(me, i + jnp.where(i >= me, 1, 0), mine)))
 
 
 def relate_kernel(q_v, bank, rel_hbm, bank_hbm, rel_v, sem):

time: 19.4 us -> 18.7 us (0.964)
  Pallas kernels: 18.6 us -> 17.9 us
    pallas_call x1, Pallas kernels: 17.4 us -> 16.7 us  [per_device(): pl.pallas_call(functools.partial(line_kernel if short else refresh_kernel...]
where the time goes in v3:
time: 18.7 us; the launch traced here: 18.6 us
  Pallas kernels  17.9 us (96%)
  between operations  0.64 us (3%)
    pallas_call x1, Pallas kernels, per_device(): pl.pallas_call(functools.partial(line_kernel if short else refresh_kernel...  16.7 us
    pallas_call x1, Pallas kernels, per_device(): pl.pallas_call(relate_kernel, out_shape=(jax.ShapeDtypeStruct((group, tok...  1.19 us

profile of v3, /device:TPU:0, one launch (start us, length us, event | category | flops | bytes accessed | tf_op | source)
XLA Modules:
  0.0 18.6 jit_solution(13712904860549927512)
XLA Ops:
  0.6 16.7 %refresh.1 = (bf16[7,128,128]{2,1,0:T(8,128)(2,1)S(1)}, bf16[512,128]{1,0:T(8,128)(2,1)S(1)}) custom-call(s32[8]{0:T(128)} %start_hbm.1, s32[1,8]{1,0:T(1,128)} %bitcast.9, bf16[7,128,128]{2,1,0:T(8,128)(2,1)} %bitcast.6, bf16[128,128]{1,0:T(8,128)(2,1)} %bitcast.7, bf16[64,128]{1,0:T(8,128)(2,1)} %bitcast.8), custom_call_target="tpu_custom_call" | custom-call | tf_op jit(solution)/shard_map/refresh/pallas_call | solution.py:519
  17.4 1.2 %relate.1 = (bf16[7,128,512]{2,1,0:T(8,128)(2,1)}, bf16[64,128]{1,0:T(8,128)(2,1)}) custom-call(bf16[7,128,128]{2,1,0:T(8,128)(2,1)S(1)} %get-tuple-element.6.q_v, bf16[512,128]{1,0:T(8,128)(2,1)S(1)} %get-tuple-element.7.bank), custom_call_target="tpu_custom_call" | custom-call | tf_op jit(solution)/shard_map/relate/pallas_call | solution.py:548

commit v4 on v3

--- a/solution.py
+++ b/solution.py
@@ -146,6 +146,7 @@
 
 
 FAR = [2, 9]
+COMPUTE_AT = [2, 3, 4, 5, 6]
 UP = [(3,), ()]
 CUP = [(1, 2, 3), ()]
 DOWN = [(), ()]
@@ -210,10 +211,6 @@
     load_w = pltpu.make_async_copy(start_hbm, start_ref, load_sem.at[3])
     load_s = pltpu.make_async_copy(slot_hbm, slot_ref, load_sem.at[4])
     load_k.start()
-    load_q.start()
-    load_c.start()
-    load_w.start()
-    load_s.start()
 
     barrier = pltpu.get_barrier_semaphore()
 
@@ -247,6 +244,11 @@
     both = [set(a) | set(b) | set(c) for a, b, c in zip(UP, DOWN, CUP)]
     for dist in range(1, rows):
         diagonal(both, dist, side == 0, lambda: signal(barrier, me + 2 * dist + 1))
+
+    load_q.start()
+    load_c.start()
+    load_w.start()
+    load_s.start()
 
     count = row + side
     for g in range(2):
@@ -433,7 +435,7 @@
         key_copy(owner, owner, ks_sem.at[owner]).wait_recv()
         relays(step, lambda copy: copy.start())
         caches(step)
-        if step >= 3 - 1:
+        if step in COMPUTE_AT:
             for at in range(done, step + 1):
                 partial(block(at)[0])
             done = step + 1

time: 18.7 us -> 18.7 us (level)
  no operation moved by 1% of the time
where the time goes in v4:
time: 18.7 us; the launch traced here: 18.6 us
  Pallas kernels  17.9 us (96%)
  between operations  0.64 us (3%)
    pallas_call x1, Pallas kernels, per_device(): pl.pallas_call(functools.partial(line_kernel if short else refresh_kernel...  16.7 us
    pallas_call x1, Pallas kernels, per_device(): pl.pallas_call(relate_kernel, out_shape=(jax.ShapeDtypeStruct((group, tok...  1.19 us

profile of v4, /device:TPU:0, one launch (start us, length us, event | category | flops | bytes accessed | tf_op | source)
XLA Modules:
  0.0 18.6 jit_solution(9383987604503451310)
XLA Ops:
  0.6 16.7 %refresh.1 = (bf16[7,128,128]{2,1,0:T(8,128)(2,1)S(1)}, bf16[512,128]{1,0:T(8,128)(2,1)S(1)}) custom-call(s32[8]{0:T(128)} %start_hbm.1, s32[1,8]{1,0:T(1,128)} %bitcast.9, bf16[7,128,128]{2,1,0:T(8,128)(2,1)} %bitcast.6, bf16[128,128]{1,0:T(8,128)(2,1)} %bitcast.7, bf16[64,128]{1,0:T(8,128)(2,1)} %bitcast.8), custom_call_target="tpu_custom_call" | custom-call | tf_op jit(solution)/shard_map/refresh/pallas_call | solution.py:521
  17.4 1.2 %relate.1 = (bf16[7,128,512]{2,1,0:T(8,128)(2,1)}, bf16[64,128]{1,0:T(8,128)(2,1)}) custom-call(bf16[7,128,128]{2,1,0:T(8,128)(2,1)S(1)} %get-tuple-element.6.q_v, bf16[512,128]{1,0:T(8,128)(2,1)S(1)} %get-tuple-element.7.bank), custom_call_target="tpu_custom_call" | custom-call | tf_op jit(solution)/shard_map/relate/pallas_call | solution.py:550

commit v5 on v3

--- a/solution.py
+++ b/solution.py
@@ -483,17 +483,24 @@
 def relate_kernel(q_v, bank, rel_hbm, bank_hbm, rel_v, sem):
     group, toks, dim = q_v.shape
     local = bank_hbm.shape[0]
+    half = toks // 2
     scale = 1.0 / math.sqrt(dim)
     first = pl.multiple_of(lax.axis_index("seq") * local, local)
-    keep = pltpu.make_async_copy(bank.at[pl.ds(first, local)], bank_hbm, sem.at[group])
+    keep = pltpu.make_async_copy(bank.at[pl.ds(first, local)], bank_hbm, sem.at[2 * group])
     keep.start()
     outs = [
-        pltpu.make_async_copy(rel_v.at[j], rel_hbm.at[j], sem.at[j]) for j in range(group)
+        pltpu.make_async_copy(
+            rel_v.at[j, pl.ds(h * half, half)], rel_hbm.at[j, pl.ds(h * half, half)], sem.at[2 * j + h]
+        )
+        for j in range(group)
+        for h in range(2)
     ]
     for j in range(group):
-        r = lax.dot_general(q_v[j], bank[...], NT, preferred_element_type=jnp.float32)
-        rel_v[j] = (r * scale).astype(jnp.bfloat16)
-        outs[j].start()
+        for h in range(2):
+            part = slice(h * half, (h + 1) * half)
+            r = lax.dot_general(q_v[j, part, :], bank[...], NT, preferred_element_type=jnp.float32)
+            rel_v[j, part, :] = (r * scale).astype(jnp.bfloat16)
+            outs[2 * j + h].start()
     for out in outs:
         out.wait()
     keep.wait()
@@ -507,7 +514,7 @@
     hbm_spec = pl.BlockSpec(memory_space=pltpu.HBM)
     vmem_spec = pl.BlockSpec(memory_space=pltpu.VMEM)
     bf16 = jnp.bfloat16
-    short = n % 2 == 0 and n <= 8
+    short = n == len(HAND_UP) * 2 + 2
     sems = [pltpu.SemaphoreType.DMA((n,))] * 6
     if short:
         sems = (
@@ -555,7 +562,7 @@
         out_specs=(hbm_spec, hbm_spec),
         scratch_shapes=[
             pltpu.VMEM((group, toks, slots), bf16),
-            pltpu.SemaphoreType.DMA((group + 1,)),
+            pltpu.SemaphoreType.DMA((2 * group + 1,)),
         ],
         compiler_params=pltpu.CompilerParams(
             vmem_limit_bytes=2 * group * toks * slots + 16 * 1024 * 1024

time: 18.7 us -> 19.1 us (1.021)
  Pallas kernels: 17.9 us -> 18.3 us
    pallas_call x1, Pallas kernels: 1.19 us -> 1.53 us  [per_device(): pl.pallas_call(relate_kernel, out_shape=(jax.ShapeDtypeStruct((group, tok...]
where the time goes in v5:
time: 19.1 us; the launch traced here: 18.9 us
  Pallas kernels  18.3 us (96%)
  between operations  0.64 us (3%)
    pallas_call x1, Pallas kernels, per_device(): pl.pallas_call(functools.partial(line_kernel if short else refresh_kernel...  16.7 us
    pallas_call x1, Pallas kernels, per_device(): pl.pallas_call(relate_kernel, out_shape=(jax.ShapeDtypeStruct((group, tok...  1.53 us

profile of v5, /device:TPU:0, one launch (start us, length us, event | category | flops | bytes accessed | tf_op | source)
XLA Modules:
  0.0 18.9 jit_solution(5721476630360789177)
XLA Ops:
  0.6 16.7 %refresh.1 = (bf16[7,128,128]{2,1,0:T(8,128)(2,1)S(1)}, bf16[512,128]{1,0:T(8,128)(2,1)S(1)}) custom-call(s32[8]{0:T(128)} %start_hbm.1, s32[1,8]{1,0:T(1,128)} %bitcast.9, bf16[7,128,128]{2,1,0:T(8,128)(2,1)} %bitcast.6, bf16[128,128]{1,0:T(8,128)(2,1)} %bitcast.7, bf16[64,128]{1,0:T(8,128)(2,1)} %bitcast.8), custom_call_target="tpu_custom_call" | custom-call | tf_op jit(solution)/shard_map/refresh/pallas_call | solution.py:526
  17.4 1.5 %relate.1 = (bf16[7,128,512]{2,1,0:T(8,128)(2,1)}, bf16[64,128]{1,0:T(8,128)(2,1)}) custom-call(bf16[7,128,128]{2,1,0:T(8,128)(2,1)S(1)} %get-tuple-element.6.q_v, bf16[512,128]{1,0:T(8,128)(2,1)S(1)} %get-tuple-element.7.bank), custom_call_target="tpu_custom_call" | custom-call | tf_op jit(solution)/shard_map/relate/pallas_call | solution.py:555
